TPU v7x, 32 devices: a whole 2x2x4 slice. The times are simulated.
32 devices in a mesh: bank: 4 (over x, core), zero: 8 (over z, y).
Axes of the slice: x: 2, y: 2, z: 4, core: 2. Of those that a mesh axis runs over, the one named last changes fastest.
Arguments:
- w_gate: float32 [64, 2048, 1024], P('bank', 'zero'), may hold values from -0.1875 to 0.1875
- avg_gate: float32 [64, 2048, 1024], P('bank', 'zero'), may hold values from -0.125 to 0.125
- w_up: float32 [64, 2048, 1024], P('bank', 'zero'), may hold values from -0.1875 to 0.1875
- avg_up: float32 [64, 2048, 1024], P('bank', 'zero'), may hold values from -0.125 to 0.125
- mix_share: float32 [64], P('bank'), may hold values from 0.2 to 0.8
- router_weight: float32 [2048, 64], P('zero', 'bank'), may hold values from -0.125 to 0.125
- router_gain: float32 [2048], P('zero'), may hold values from 0.25 to 1.75
Outputs:
- serve_gate: bfloat16 [64, 2048, 1024], P('bank', None, 'zero')
- serve_up: bfloat16 [64, 2048, 1024], P('bank', None, 'zero')
- scale_gate: float32 [64, 1024], P('bank', 'zero')
- scale_up: float32 [64, 1024], P('bank', 'zero')
- serve_router: bfloat16 [2048, 64], replicated
All inputs are finite; a program needn't handle non-finite values. Where the computation divides by a largest or mean magnitude, that divisor is 1e-20 or more.
Results may differ from a plain program's by a relative error of at most 0.001.
Values may be sent and summed in bfloat16 or wider, within the bound.
A program may use at most 256 MiB of HBM per device.

v0:
```python
import jax
import jax.numpy as jnp
from jax import lax
from jax.sharding import PartitionSpec as P

D_MODEL = 2048


def on_device(w_gate, avg_gate, w_up, avg_up, mix_share, router_weight, router_gain):
    fresh_gate = mix_share[:, None, None] * w_gate + (1.0 - mix_share[:, None, None]) * avg_gate
    fresh_up = mix_share[:, None, None] * w_up + (1.0 - mix_share[:, None, None]) * avg_up
    total_gate, total_up = lax.psum(
        (jnp.sum(jnp.abs(fresh_gate), axis=1), jnp.sum(jnp.abs(fresh_up), axis=1)), "zero"
    )
    scale_gate = total_gate / D_MODEL
    scale_up = total_up / D_MODEL
    narrow_gate, narrow_up = (
        (fresh_gate / jnp.expand_dims(scale_gate, 1)).astype(jnp.bfloat16),
        (fresh_up / jnp.expand_dims(scale_up, 1)).astype(jnp.bfloat16),
    )
    serve_gate, serve_up = (
        lax.all_to_all(narrow_gate, "zero", split_axis=2, concat_axis=1, tiled=True),
        lax.all_to_all(narrow_up, "zero", split_axis=2, concat_axis=1, tiled=True),
    )
    scale_gate = lax.dynamic_slice_in_dim(
        scale_gate, lax.axis_index("zero") * serve_gate.shape[2], serve_gate.shape[2], axis=1
    )
    scale_up = lax.dynamic_slice_in_dim(
        scale_up, lax.axis_index("zero") * serve_up.shape[2], serve_up.shape[2], axis=1
    )
    part_router = (router_weight * router_gain[:, None]).astype(jnp.bfloat16)
    row_router = lax.all_gather(part_router, "zero", axis=0, tiled=True)
    serve_router = lax.all_gather(row_router, "bank", axis=1, tiled=True)
    return (serve_gate, serve_up, scale_gate, scale_up, serve_router)


def solution(mesh):
    in_specs = (
        P("bank", "zero", None),
        P("bank", "zero", None),
        P("bank", "zero", None),
        P("bank", "zero", None),
        P("bank"),
        P("zero", "bank"),
        P("zero"),
    )
    out_specs = (
        P("bank", None, "zero"),
        P("bank", None, "zero"),
        P("bank", "zero"),
        P("bank", "zero"),
        P(),
    )
    return jax.shard_map(
        on_device, mesh=mesh, in_specs=in_specs, out_specs=out_specs, check_vma=False
    )
```

profile of v0, /device:TPU:12, one launch (start us, length us, event | category | flops | bytes accessed | tf_op | source)
XLA Modules:
  0.0 638.0 jit_solution(310486662684483789)
XLA Ops:
  7.2 0.0 all-reduce.3.cloned.1.call-start
  7.2 17.6 %copy.22 = f32[16,256,1024]{1,0,2:T(8,128)} copy(f32[16,256,1024]{2,1,0:T(8,128)} %param.7) | data formatting | bytes 33554432 | tf_op args[0]
  24.8 17.6 %copy.23 = f32[16,256,1024]{1,0,2:T(8,128)} copy(f32[16,256,1024]{2,1,0:T(8,128)} %param.8) | data formatting | bytes 33554432 | tf_op args[1]
  42.4 17.6 %copy.25 = f32[16,256,1024]{1,0,2:T(8,128)} copy(f32[16,256,1024]{2,1,0:T(8,128)} %param.9) | data formatting | bytes 33554432 | tf_op args[2]
  60.0 0.0 copy-start.1
  60.0 17.6 %copy.26 = f32[16,256,1024]{1,0,2:T(8,128)} copy(f32[16,256,1024]{2,1,0:T(8,128)} %param.10) | data formatting | bytes 33554432 | tf_op args[3]
  77.6 0.0 copy-done.1
  77.6 23.7 %abs_reduce_fusion = (f32[16,1024]{0,1:T(8,128)}, f32[16,1024]{0,1:T(8,128)}) fusion(f32[16,256,1024]{1,0,2:T(8,128)} %copy.26, f32[16]{0:T(128)S(1)} %broadcast_subtract_fusion, f32[16,256,1024]{1,0,2:T(8,128)} %copy.25, f32[16]{0:T(128)S(1)} %copy-done.1, f32[16,256,1024]{1,0,2:T(8,128)} %copy.23, f32[16,256,1024]{1,0,2:T(8,128)} %copy.22), kind=kLoop, calls=%fused_computation.1 | loop fusion | flops 41910272 | bytes 67240064 | tf_op jit(solution)/shard_map/reduce_sum | solution.py:13
  101.3 0.0 all-reduce.3.cloned.1.call-update
  101.4 79.1 %all-reduce.3.cloned.1.call-done = (f32[16,1024]{0,1:T(8,128)}, f32[16,1024]{0,1:T(8,128)}) async-done(((f32[16,1024]{0,1:T(8,128)}, f32[16,1024]{0,1:T(8,128)}), (f32[16,1024]{0,1:T(8,128)}, f32[16,1024]{0,1:T(8,128)})) %all-reduce.3.cloned.1.call-update) | async-done | bytes 131088 | tf_op jit(solution)/shard_map/psum | solution.py:12
  180.4 1.3 broadcast_multiply_fusion
  181.7 25.3 %divide_convert_fusion = (bf16[16,256,1024]{1,0,2:T(8,128)(2,1)}, bf16[16,256,1024]{1,0,2:T(8,128)(2,1)S(1)}) fusion(f32[16,1024]{0,1:T(8,128)S(1)} %get-tuple-element.16, f32[16,256,1024]{1,0,2:T(8,128)} %copy.26, f32[16]{0:T(128)S(1)} %broadcast_subtract_fusion, f32[16,256,1024]{1,0,2:T(8,128)} %copy.25, f32[16]{0:T(128)S(1)} %copy-done.1, ...), kind=kLoop, calls=%fused_computation | loop fusion | flops 41943040 | bytes 84017280 | tf_op jit(solution)/shard_map/convert_element_type | solution.py:19
  207.0 0.0 copy-start
  207.0 0.0 copy-start.2
  207.0 186.0 %all_to_all.36 = bf16[16,256,1024]{1,0,2:T(8,128)(2,1)} all-to-all(bf16[16,256,1024]{1,0,2:T(8,128)(2,1)S(1)} %get-tuple-element.15), channel_id=1, replica_groups=mesh['bank'=4,'zero'=8] {'zero'}, dimensions={2} | all-to-all | bytes 16777216 | tf_op jit(solution)/shard_map/all_to_all | solution.py:22
  393.1 6.8 %all-to-all-start.1 = ((bf16[16,256,1024]{1,0,2:T(8,128)(2,1)}), bf16[16,256,1024]{1,0,2:T(8,128)(2,1)}, u32[]{:S(2)}, u32[]{:S(2)}) async-start(bf16[16,256,1024]{1,0,2:T(8,128)(2,1)} %get-tuple-element.14), calls=%async_computation.1 | async-start | bytes 16777216 | tf_op jit(solution)/shard_map/all_to_all | solution.py:23
  399.9 0.0 copy-done
  399.9 0.0 copy-done.2
  399.9 198.9 %all_gather.6 = bf16[2048,16]{0,1:T(8,128)(2,1)S(1)} all-gather(bf16[256,16]{0,1:T(8,128)(2,1)S(1)} %multiply_convert_fusion), channel_id=1, replica_groups=mesh['bank'=4,'zero'=8] {'zero'}, dimensions={0}, use_global_device_ids=true | all-gather | bytes 73728 | tf_op jit(solution)/shard_map/all_gather | solution.py:32
  598.8 5.8 all_gather.7
  604.6 0.7 copy.28
  605.3 0.7 copy.29
  605.9 12.3 %copy.24 = bf16[16,8,256,128]{3,2,1,0:T(8,128)(2,1)} copy(bf16[16,8,256,128]{2,0,3,1:T(8,128)(2,1)} %bitcast.8) | data formatting | bytes 16777216 | tf_op jit(solution)/shard_map/all_to_all | solution.py:22
  618.2 0.0 all-to-all-done.1
  618.2 12.3 %copy.27 = bf16[16,8,256,128]{3,2,1,0:T(8,128)(2,1)} copy(bf16[16,8,256,128]{2,0,3,1:T(8,128)(2,1)} %bitcast.4) | data formatting | bytes 16777216 | tf_op jit(solution)/shard_map/all_to_all | solution.py:23
  630.5 0.7 copy.33
  (4 shorter events, 0.0 us)
Async XLA Ops:
  7.2 173.3 %all-reduce.3.cloned.1.call-start = ((), (), s32[]{:S(2)}) async-start(), calls=%async_computation.2 | async-start | bytes 2097152 | tf_op jit(solution)/shard_map/psum | solution.py:12
  60.0 17.6 %copy-start.1 = (f32[16]{0:T(128)S(1)}, f32[16]{0:T(128)}, u32[]{:S(2)}) copy-start(f32[16]{0:T(128)} %param.11) | copy-start | bytes 196
  207.0 192.9 %copy-start = (f32[256,16]{0,1:T(8,128)S(1)}, f32[256,16]{0,1:T(8,128)}, u32[]{:S(2)}) copy-start(f32[256,16]{0,1:T(8,128)} %param.12) | copy-start | bytes 49156
  207.0 192.9 %copy-start.2 = (f32[256]{0:T(256)S(1)}, f32[256]{0:T(256)}, u32[]{:S(2)}) copy-start(f32[256]{0:T(256)} %param.13) | copy-start | bytes 3076
  393.1 225.1 %all-to-all-start.1 = ((bf16[16,256,1024]{1,0,2:T(8,128)(2,1)}), bf16[16,256,1024]{1,0,2:T(8,128)(2,1)}, u32[]{:S(2)}, u32[]{:S(2)}) async-start(bf16[16,256,1024]{1,0,2:T(8,128)(2,1)} %get-tuple-element.14), calls=%async_computation.1 | async-start | bytes 16777216 | tf_op jit(solution)/shard_map/all_to_all | solution.py:23
Sparse Core Ops, SparseCore 0:
  101.5 78.9 all-reduce.2
where the time goes:
time: 644 us; the launch traced here: 638 us
  blocking collectives  391 us (61%)
  local copies, waits for them, and re-layouts  97 us (15%)
  waiting for transfers between devices  79.1 us (12%)
  other arithmetic  50.3 us (8%)
  between operations  14.1 us (2%)
  starting transfers between devices  6.87 us (1%)
    all_gather x1, blocking collectives, on_device(): row_router = lax.all_gather(part_router, 'zero', axis=0, tiled=True)  199 us
    all_to_all x1, blocking collectives, on_device(): lax.all_to_all(narrow_gate, 'zero', split_axis=2, concat_axis=1, tiled=True)  186 us
    psum x1, waiting for transfers between devices, on_device(): lax.psum((jnp.sum(jnp.abs(fresh_gate), axis=1), jnp.sum(jnp.abs(fresh_up)...  79.1 us
    unnamed x13, local copies, waits for them, and re-layouts  72.5 us
    convert_element_type x1, other arithmetic, on_device(): (fresh_up / jnp.expand_dims(scale_up, 1)).astype(jnp.bfloat16)  25.3 us
    reduce_sum x1, other arithmetic, on_device(): jnp.sum(jnp.abs(fresh_up), axis=1)  23.7 us
  transfers between devices with their start and end apart: 2, of which 1 were waited for; matrix products, arithmetic and copies ran while one was open for 2% of the time, Pallas kernels for 0%

commit v1 on v0

v1 whole, which is shorter than its diff:
```python
import functools

import jax
import jax.numpy as jnp
from jax import lax
from jax.experimental import pallas as pl
from jax.experimental.pallas import tpu as pltpu
from jax.sharding import PartitionSpec as P

MESH = pl.DeviceIdType.MESH
SLOTS = 4


def partner(me, k, n):
    out, bit = me, 1
    while bit < n:
        if k & bit:
            out = out + bit * (1 - 2 * ((me // bit) % 2))
        bit *= 2
    return out


def plan(experts):
    first = max(1, experts // 8)
    sizes = [first, first, experts - 2 * first]
    groups, at, row = [], 0, 0
    for i, size in enumerate(sizes):
        if i == 0:
            cuts = [size]
        elif i == 1:
            cuts = [size // 2, size - size // 2]
        else:
            step = max(1, size // 3)
            cuts = [step, step, size - 2 * step]
        pieces, p = [], at
        for c in cuts:
            if c > 0:
                pieces.append((p, c))
                p += c
        rows = -(-2 * size // 8) * 8
        groups.append((at, size, row, rows, pieces))
        at += size
        row += rows
    return groups, row


def kernel(
    nz, nb, groups,
    mix, wg, ag, wu, au, rw, gain,
    og, ou, sg, su, rt,
    fresh, stage, send, part, rs, scl, rtp,
    in_sem, bulk_ssem, bulk_rsem, own_sem, rs_ssem, rs_rsem, ag_ssem, ag_rsem,
    r1_ssem, r1_rsem, r2_ssem, r2_rsem, r_own,
):
    me = lax.axis_index("zero")
    bank = lax.axis_index("bank")
    experts, rows, _ = wg.shape
    cb = part.shape[2]
    eb = rw.shape[0]
    ws, avgs, outs, scales = (wg, wu), (ag, au), (og, ou), (sg, su)
    peers = [partner(me, k, nz) for k in range(1, nz)]
    banks = [partner(bank, k, nb) for k in range(1, nb)]

    def loads(e):
        slot = lax.rem(e, SLOTS)
        out = []
        for m in range(2):
            out.append(pltpu.make_async_copy(ws[m].at[e], fresh.at[m, e], in_sem.at[slot, m, 0]))
            out.append(pltpu.make_async_copy(avgs[m].at[e], stage.at[slot, m], in_sem.at[slot, m, 1]))
        return out

    for e in range(min(SLOTS, experts)):
        for c in loads(e):
            c.start()

    barrier = pltpu.get_barrier_semaphore()
    for p in peers:
        pl.semaphore_signal(barrier, inc=1, device_id={"zero": p}, device_id_type=MESH)
    for p in banks:
        pl.semaphore_signal(barrier, inc=1, device_id={"bank": p}, device_id_type=MESH)

    part[...] = jnp.zeros_like(part)
    rtp[...] = (rw[...] * gain[...]).astype(rtp.dtype)

    def compute(g):
        at, size, row0, _, _ = groups[g]

        def body(e, carry):
            slot = lax.rem(e, SLOTS)
            for c in loads(e):
                c.wait()
            a = mix[e]
            b = 1.0 - a
            for m in range(2):
                row = row0 + m * size + (e - at)
                for d in range(nz):
                    cols = slice(d * cb, (d + 1) * cb)
                    v = a * fresh[m, e, :, cols] + b * stage[slot, m, :, cols]
                    fresh[m, e, :, cols] = v
                    part[d, pl.ds(row, 1), :] = jnp.sum(jnp.abs(v), axis=0, keepdims=True)

            @pl.when(e + SLOTS < experts)
            def _():
                for c in loads(e + SLOTS):
                    c.start()

            return carry

        lax.fori_loop(at, at + size, body, 0)

    def scatter(g):
        _, _, row0, n, _ = groups[g]
        span = pl.ds(row0, n)
        out = []
        for k, p in enumerate(peers):
            out.append(pltpu.make_async_remote_copy(
                part.at[p, span], rs.at[k, span], rs_ssem.at[g, k], rs_rsem.at[g, k],
                device_id={"zero": p}, device_id_type=MESH))
            out[-1].start()
        return out

    def gather(g, pending):
        at, size, row0, n, _ = groups[g]
        span = pl.ds(row0, n)
        for c in pending:
            c.wait()
        total = part[me, span, :]
        for k in range(nz - 1):
            total = total + rs[k, span, :]
        total = total / (rows * nz)
        scl[me, span, :] = total
        for m in range(2):
            scales[m][at:at + size, :] = total[m * size:(m + 1) * size, :]
        out = []
        for k, p in enumerate(peers):
            out.append(pltpu.make_async_remote_copy(
                scl.at[me, span], scl.at[me, span], ag_ssem.at[g, k], ag_rsem.at[g, k],
                device_id={"zero": p}, device_id_type=MESH))
            out[-1].start()
        return out

    def narrow(g, lo, n):
        at, size, row0, _, _ = groups[g]

        def body(e, carry):
            for m in range(2):
                row = row0 + m * size + (e - at)
                for d in range(nz):
                    cols = slice(d * cb, (d + 1) * cb)
                    inverse = 1.0 / scl[d, pl.ds(row, 1), :]
                    send[m, d, e] = (fresh[m, e, :, cols] * inverse).astype(send.dtype)
            return carry

        lax.fori_loop(lo, lo + n, body, 0)

    place = pl.ds(pl.multiple_of(me * rows, rows), rows)
    flying = []
    count = [0]

    def push(lo, n):
        i = count[0]
        count[0] += 1
        span = pl.ds(lo, n)
        for k, p in enumerate(peers):
            for m in range(2):
                c = pltpu.make_async_remote_copy(
                    send.at[m, p, span], outs[m].at[span, place], bulk_ssem.at[i, m, k], bulk_rsem.at[i, m, k],
                    device_id={"zero": p}, device_id_type=MESH)
                c.start()
                flying.append(c)
        for m in range(2):
            c = pltpu.make_async_copy(send.at[m, me, span], outs[m].at[span, place], own_sem.at[i, m])
            c.start()
            flying.append(c)

    compute(0)
    pl.semaphore_wait(barrier, nz - 1 + nb - 1)
    rs0 = scatter(0)
    band = pl.ds(pl.multiple_of(bank * eb, eb), eb)
    if len(rt.shape) == 2:
        mine, column = rt.at[band, place], rt.at[band]
    else:
        mine, column = rt.at[me, band], rt.at[:, band]
    first = []
    for k, p in enumerate(peers):
        first.append(pltpu.make_async_remote_copy(
            rtp, mine, r1_ssem.at[k], r1_rsem.at[k], device_id={"zero": p}, device_id_type=MESH))
    first.append(pltpu.make_async_copy(rtp, mine, r_own))
    compute(1)
    rs1 = scatter(1)
    ag0 = gather(0, rs0)
    ag1 = gather(1, rs1)
    for c in first:
        c.start()
    for c in ag0:
        c.wait()
    for lo, n in groups[0][4]:
        narrow(0, lo, n)
        push(lo, n)
    compute(2)
    rs2 = scatter(2)
    for c in ag1:
        c.wait()
    pieces = groups[1][4]
    narrow(1, *pieces[0])
    push(*pieces[0])
    for lo, n in pieces[1:]:
        narrow(1, lo, n)
    for c in first:
        c.wait()
    for k, p in enumerate(banks):
        c = pltpu.make_async_remote_copy(
            column, column, r2_ssem.at[k], r2_rsem.at[k], device_id={"bank": p}, device_id_type=MESH)
        c.start()
        flying.append(c)
    ag2 = gather(2, rs2)
    for lo, n in pieces[1:]:
        push(lo, n)
    for c in ag2:
        c.wait()
    for lo, n in groups[2][4]:
        narrow(2, lo, n)
        push(lo, n)
    for c in flying:
        c.wait()


def solution(mesh):
    nz, nb = mesh.shape["zero"], mesh.shape["bank"]

    def on_device(w_gate, avg_gate, w_up, avg_up, mix_share, router_weight, router_gain):
        experts, rows, columns = w_gate.shape
        cb = columns // nz
        eb = router_weight.shape[1]
        groups, stat = plan(experts)
        npieces = sum(len(g[4]) for g in groups)
        anyspace = pl.BlockSpec(memory_space=pl.ANY)
        vmem = pl.BlockSpec(memory_space=pltpu.VMEM)
        dma = pltpu.SemaphoreType.DMA
        out = jax.ShapeDtypeStruct((experts, rows * nz, cb), jnp.bfloat16)
        scale = jax.ShapeDtypeStruct((experts, cb), jnp.float32)
        flat = rows % 128 == 0
        router = (eb * nb, rows * nz) if flat else (nz, eb * nb, rows)
        router = jax.ShapeDtypeStruct(router, jnp.bfloat16)
        ng = len(groups)
        sg, su, cg, cu, rt = pl.pallas_call(
            functools.partial(kernel, nz, nb, groups),
            out_shape=(out, out, scale, scale, router),
            in_specs=[pl.BlockSpec(memory_space=pltpu.SMEM)] + [anyspace] * 4 + [vmem] * 2,
            out_specs=(anyspace, anyspace, vmem, vmem, anyspace),
            scratch_shapes=[
                pltpu.VMEM((2, experts, rows, columns), jnp.float32),
                pltpu.VMEM((SLOTS, 2, rows, columns), jnp.float32),
                pltpu.VMEM((2, nz, experts, rows, cb), jnp.bfloat16),
                pltpu.VMEM((nz, stat, cb), jnp.float32),
                pltpu.VMEM((nz - 1, stat, cb), jnp.float32),
                pltpu.VMEM((nz, stat, cb), jnp.float32),
                pltpu.VMEM((eb, rows), jnp.bfloat16),
                dma((SLOTS, 2, 2)),
                dma((npieces, 2, nz - 1)),
                dma((npieces, 2, nz - 1)),
                dma((npieces, 2)),
                dma((ng, nz - 1)),
                dma((ng, nz - 1)),
                dma((ng, nz - 1)),
                dma((ng, nz - 1)),
                dma((nz - 1,)),
                dma((nz - 1,)),
                dma((nb - 1,)),
                dma((nb - 1,)),
                dma,
            ],
            compiler_params=pltpu.CompilerParams(
                collective_id=0, has_side_effects=True, vmem_limit_bytes=67_000_000
            ),
        )(mix_share, w_gate, avg_gate, w_up, avg_up, router_weight.T, router_gain[None, :])
        rt = rt.T if flat else rt.transpose(0, 2, 1).reshape(nz * rows, nb * eb)
        return sg, su, cg, cu, rt

    in_specs = (
        P("bank", "zero", None),
        P("bank", "zero", None),
        P("bank", "zero", None),
        P("bank", "zero", None),
        P("bank"),
        P("zero", "bank"),
        P("zero"),
    )
    out_specs = (
        P("bank", None, "zero"),
        P("bank", None, "zero"),
        P("bank", "zero"),
        P("bank", "zero"),
        P(),
    )
    return jax.shard_map(
        on_device, mesh=mesh, in_specs=in_specs, out_specs=out_specs, check_vma=False
    )
```

time: 644 us -> 402 us (0.62)
  blocking collectives: 391 us -> 0 us
  Pallas kernels: 0 us -> 384 us
  local copies, waits for them, and re-layouts: 97 us -> 17.1 us
  waiting for transfers between devices: 79.1 us -> 0 us
  other arithmetic: 50.3 us -> 0 us
  between operations: 14.1 us -> 0.67 us
  starting transfers between devices: 6.87 us -> 0 us
    pallas_call x0 -> x1, Pallas kernels: none -> 384 us  [on_device(): pl.pallas_call(functools.partial(kernel, nz, nb, groups), out_shape=(out,...]
    all_gather x2 -> x0, blocking collectives: 205 us -> none  [the longest x1 199 us: on_device(): row_router = lax.all_gather(part_router, 'zero', axis=0, tiled=True)]
    all_to_all x1 -> x0, blocking collectives: 186 us -> none  [on_device(): lax.all_to_all(narrow_gate, 'zero', split_axis=2, concat_axis=1, tiled=True)]
    psum x1 -> x0, waiting for transfers between devices: 79.1 us -> none  [on_device(): lax.psum((jnp.sum(jnp.abs(fresh_gate), axis=1), jnp.sum(jnp.abs(fresh_up)...]
    unnamed x13 -> x11, local copies, waits for them, and re-layouts: 72.5 us -> 17.1 us
    convert_element_type x2 -> x0, other arithmetic: 25.3 us -> none  [the longest x1 25.3 us: on_device(): (fresh_up / jnp.expand_dims(scale_up, 1)).astype(jnp.bfloat16)]
    all_to_all x2 -> x0, local copies, waits for them, and re-layouts: 24.6 us -> none  [the longest x1 12.3 us: on_device(): lax.all_to_all(narrow_up, 'zero', split_axis=2, concat_axis=1, tiled=True)]
    reduce_sum x1 -> x0, other arithmetic: 23.7 us -> none  [on_device(): jnp.sum(jnp.abs(fresh_up), axis=1)]
  transfers between devices with their start and end apart: 2 -> 0, of which waited for: 1 -> 0; matrix products, arithmetic and copies ran while one was open for 2% -> 0% of each run, Pallas kernels for 0% -> 0%
where the time goes in v1:
time: 402 us
  Pallas kernels  384 us (96%)
  local copies, waits for them, and re-layouts  17.1 us (4%)
    pallas_call x1, Pallas kernels, on_device(): pl.pallas_call(functools.partial(kernel, nz, nb, groups), out_shape=(out,...  384 us
    unnamed x11, local copies, waits for them, and re-layouts  17.1 us

profile of v1, /device:TPU:12, one launch (start us, length us, event | category | flops | bytes accessed | tf_op | source)
XLA Modules:
  0.0 401.5 jit_solution(9857677369391515241)
XLA Ops:
  0.6 383.7 %shard_map.110 = (bf16[16,2048,128]{2,1,0:T(8,128)(2,1)}, bf16[16,2048,128]{2,1,0:T(8,128)(2,1)}, f32[16,128]{1,0:T(8,128)}, f32[16,128]{1,0:T(8,128)}, bf16[64,2048]{1,0:T(8,128)(2,1)}) custom-call(f32[16]{0:T(128)} %mix.1, f32[16,256,1024]{2,1,0:T(8,128)} %wg.1, f32[16,256,1024]{2,1,0:T(8,128)} %ag.1, f32[16,256,1024]{2,1,0:T(8,128)} %wu.1, ...), custom_call_target="tpu_custom_call" | custom-call | tf_op jit(solution)/shard_map/pallas_call | solution.py:246
  384.3 0.0 copy-start.2
  384.4 0.0 copy-start.1
  384.4 0.0 copy-start
  384.4 7.6 %copy.17 = bf16[16,2048,128]{2,1,0:T(8,128)(2,1)} copy(bf16[16,2048,128]{2,1,0:T(8,128)(2,1)} %get-tuple-element.20) | data formatting | bytes 16777216
  392.0 7.6 %copy.18 = bf16[16,2048,128]{2,1,0:T(8,128)(2,1)} copy(bf16[16,2048,128]{2,1,0:T(8,128)(2,1)} %get-tuple-element.21) | data formatting | bytes 16777216
  399.6 0.0 copy-done.2
  399.6 0.6 copy.19
  400.2 0.0 copy-done.1
  400.2 0.6 copy.20
  400.8 0.0 copy-done
  400.8 0.7 copy.21
Async XLA Ops:
  384.3 15.2 %copy-start.2 = (f32[16,128]{1,0:T(8,128)S(1)}, f32[16,128]{1,0:T(8,128)}, u32[]{:S(2)}) copy-start(f32[16,128]{1,0:T(8,128)} %get-tuple-element.22) | copy-start | bytes 24580
  384.4 15.8 %copy-start.1 = (f32[16,128]{1,0:T(8,128)S(1)}, f32[16,128]{1,0:T(8,128)}, u32[]{:S(2)}) copy-start(f32[16,128]{1,0:T(8,128)} %get-tuple-element.23) | copy-start | bytes 24580
  384.4 16.4 %copy-start = (bf16[64,2048]{1,0:T(8,128)(2,1)S(1)}, bf16[64,2048]{1,0:T(8,128)(2,1)}, u32[]{:S(2)}) copy-start(bf16[64,2048]{1,0:T(8,128)(2,1)} %get-tuple-element.14) | copy-start | bytes 786436

commit v2 on v1

--- a/solution.py
+++ b/solution.py
@@ -21,14 +21,14 @@
 
 
 def plan(experts):
-    first = max(1, experts // 8)
-    sizes = [first, first, experts - 2 * first]
+    first = max(1, experts // 16)
+    sizes = [first, 3 * first, experts - 4 * first]
     groups, at, row = [], 0, 0
     for i, size in enumerate(sizes):
         if i == 0:
             cuts = [size]
         elif i == 1:
-            cuts = [size // 2, size - size // 2]
+            cuts = [first] * 3
         else:
             step = max(1, size // 3)
             cuts = [step, step, size - 2 * step]
@@ -197,15 +197,16 @@
     for lo, n in groups[0][4]:
         narrow(0, lo, n)
         push(lo, n)
+    for c in ag1:
+        c.wait()
+    early, middle, late = groups[1][4]
+    narrow(1, *early)
+    push(*early)
     compute(2)
     rs2 = scatter(2)
-    for c in ag1:
-        c.wait()
-    pieces = groups[1][4]
-    narrow(1, *pieces[0])
-    push(*pieces[0])
-    for lo, n in pieces[1:]:
-        narrow(1, lo, n)
+    narrow(1, *middle)
+    push(*middle)
+    narrow(1, *late)
     for c in first:
         c.wait()
     for k, p in enumerate(banks):
@@ -214,8 +215,7 @@
         c.start()
         flying.append(c)
     ag2 = gather(2, rs2)
-    for lo, n in pieces[1:]:
-        push(lo, n)
+    push(*late)
     for c in ag2:
         c.wait()
     for lo, n in groups[2][4]:
@@ -223,6 +223,26 @@
         push(lo, n)
     for c in flying:
         c.wait()
+
+
+def settle(count, *refs):
+    sources, targets, buffers = refs[:count], refs[count:2 * count], refs[2 * count:3 * count]
+    big_in, big_out, small_in, small_out = refs[3 * count:]
+    jobs = []
+    for i in range(2):
+        for e in range(sources[i].shape[0]):
+            jobs.append((sources[i].at[e], buffers[i].at[e], targets[i].at[e], big_in.at[i, e], big_out.at[i, e]))
+    for i in range(2, count):
+        jobs.append((sources[i], buffers[i], targets[i], small_in.at[i - 2], small_out.at[i - 2]))
+    reads = [pltpu.make_async_copy(src, buf, sem) for src, buf, _, sem, _ in jobs]
+    writes = [pltpu.make_async_copy(buf, dst, sem) for _, buf, dst, _, sem in jobs]
+    for r in reads:
+        r.start()
+    for r, w in zip(reads, writes):
+        r.wait()
+        w.start()
+    for w in writes:
+        w.wait()
 
 
 def solution(mesh):
@@ -243,7 +263,7 @@
         router = (eb * nb, rows * nz) if flat else (nz, eb * nb, rows)
         router = jax.ShapeDtypeStruct(router, jnp.bfloat16)
         ng = len(groups)
-        sg, su, cg, cu, rt = pl.pallas_call(
+        landed = pl.pallas_call(
             functools.partial(kernel, nz, nb, groups),
             out_shape=(out, out, scale, scale, router),
             in_specs=[pl.BlockSpec(memory_space=pltpu.SMEM)] + [anyspace] * 4 + [vmem] * 2,
@@ -274,6 +294,17 @@
                 collective_id=0, has_side_effects=True, vmem_limit_bytes=67_000_000
             ),
         )(mix_share, w_gate, avg_gate, w_up, avg_up, router_weight.T, router_gain[None, :])
+        shapes = (out, out, scale, scale, router)
+        sg, su, cg, cu, rt = pl.pallas_call(
+            functools.partial(settle, len(shapes)),
+            out_shape=shapes,
+            in_specs=[anyspace] * len(shapes),
+            out_specs=(anyspace,) * len(shapes),
+            scratch_shapes=[pltpu.VMEM(x.shape, x.dtype) for x in shapes]
+            + [dma((2, experts))] * 2
+            + [dma((len(shapes) - 2,))] * 2,
+            compiler_params=pltpu.CompilerParams(vmem_limit_bytes=60_000_000),
+        )(*landed)
         rt = rt.T if flat else rt.transpose(0, 2, 1).reshape(nz * rows, nb * eb)
         return sg, su, cg, cu, rt
 

time: 402 us -> 396 us (0.985)
  local copies, waits for them, and re-layouts: 17.1 us -> 0 us
  Pallas kernels: 384 us -> 395 us
    unnamed x11 -> x0, local copies, waits for them, and re-layouts: 17.1 us -> none
    pallas_call x0 -> x1, Pallas kernels: none -> 12.5 us  [on_device(): pl.pallas_call(functools.partial(settle, len(shapes)), out_shape=shapes,...]
where the time goes in v2:
time: 396 us
  Pallas kernels  395 us (100%)
    pallas_call x1, Pallas kernels, on_device(): pl.pallas_call(functools.partial(kernel, nz, nb, groups), out_shape=(out,...  383 us
    pallas_call x1, Pallas kernels, on_device(): pl.pallas_call(functools.partial(settle, len(shapes)), out_shape=shapes,...  12.5 us

profile of v2, /device:TPU:12, one launch (start us, length us, event | category | flops | bytes accessed | tf_op | source)
XLA Modules:
  0.0 395.8 jit_solution(10927004967650237481)
XLA Ops:
  0.6 382.7 %shard_map.110 = (bf16[16,2048,128]{2,1,0:T(8,128)(2,1)}, bf16[16,2048,128]{2,1,0:T(8,128)(2,1)}, f32[16,128]{1,0:T(8,128)}, f32[16,128]{1,0:T(8,128)}, bf16[64,2048]{1,0:T(8,128)(2,1)}) custom-call(f32[16]{0:T(128)} %mix.1, f32[16,256,1024]{2,1,0:T(8,128)} %wg.1, f32[16,256,1024]{2,1,0:T(8,128)} %ag.1, f32[16,256,1024]{2,1,0:T(8,128)} %wu.1, ...), custom_call_target="tpu_custom_call" | custom-call | tf_op jit(solution)/shard_map/pallas_call | solution.py:266
  383.3 12.5 %shard_map.111 = (bf16[16,2048,128]{2,1,0:T(8,128)(2,1)}, bf16[16,2048,128]{2,1,0:T(8,128)(2,1)}, f32[16,128]{1,0:T(8,128)}, f32[16,128]{1,0:T(8,128)}, bf16[64,2048]{1,0:T(8,128)(2,1)}) custom-call(bf16[16,2048,128]{2,1,0:T(8,128)(2,1)} %get-tuple-element.15.refs_0_, bf16[16,2048,128]{2,1,0:T(8,128)(2,1)} %get-tuple-element.16.refs_1_, ...), custom_call_target="tpu_custom_call" | custom-call | tf_op jit(solution)/shard_map/pallas_call | solution.py:298
